TPU v7x, 32 devices: a whole 2x2x4 slice. The times are simulated.
32 devices in a mesh: dp: 8 (over z, y), mp: 4 (over x, core).
Axes of the slice: x: 2, y: 2, z: 4, core: 2. Of those that a mesh axis runs over, the one named last changes fastest.
Arguments:
- tokens: bfloat16 [8, 1024, 1280], P('dp', 'mp'), may hold values from -6 to 6
- sizes: float32 [8, 1024], P('dp'), may hold values from 1 to 8
- ln1_gain: float32 [1280], replicated, may hold values from 0.25 to 1.75
- qkv_weight: bfloat16 [3, 1280, 1280], P(None, 'dp', 'mp'), may hold values from -0.15625 to 0.15625
- proj_weight: bfloat16 [1280, 1280], P('mp', 'dp'), may hold values from -0.15625 to 0.15625
- ln2_gain: float32 [1280], replicated, may hold values from 0.25 to 1.75
- fc1_weight: bfloat16 [1280, 5120], P('dp', 'mp'), may hold values from -0.15625 to 0.15625
- fc1_bias: float32 [5120], P('mp'), may hold values from -3 to 3
- fc2_weight: bfloat16 [5120, 1280], P('mp', 'dp'), may hold values from -0.078125 to 0.078125
- pair_source: int32 [8, 16], P('dp'), may hold values from 0 to 1022, as said below
- pair_target: int32 [8, 16], P('dp'), may hold values from 1 to 1023, as said below
- kept_order: int32 [8, 1008], P('dp'), may hold values from 0 to 1023, as said below
Outputs:
- merged_out: bfloat16 [8, 1008, 1280], P('dp', 'mp')
Inputs may be any that keep to these rules, and one draw needn't show every extreme that they name: `pair_source`: in each image the 16 entries are distinct even token indices. `pair_target`: odd token indices; several sources may join the same target. `kept_order`: in each image every token index that is not in pair_source appears exactly once.
All inputs are finite; a program needn't handle non-finite values.
Results may differ from a plain program's by a relative error of at most 0.017.
Values may be sent and summed in bfloat16 or wider, within the bound.
A program may use at most 64 MiB of HBM per device.

v0:
```python
import math
import jax
import jax.numpy as jnp
from jax import lax
from jax.sharding import PartitionSpec as P

D = 1280
HEADS = 16


def layer_norm(values, gain):
    center = values - jnp.mean(values, axis=-1, keepdims=True)
    spread = jnp.mean(center * center, axis=-1, keepdims=True)
    return center * lax.rsqrt(spread + 1e-06) * gain


def merge_rows(total, order_rows, source_ids, target_ids):
    kept_rows = jnp.take_along_axis(total, order_rows[:, :, None], axis=1)
    source_rows = jnp.take_along_axis(total, source_ids[:, :, None], axis=1)
    joins = (order_rows[:, :, None] == target_ids[:, None, :]).astype(jnp.float32)
    return kept_rows + jnp.einsum(
        "icr,ird->icd", joins, source_rows, precision=lax.Precision.HIGHEST
    )


def shards(
    tokens,
    sizes,
    ln1_gain,
    qkv_weight,
    proj_weight,
    ln2_gain,
    fc1_weight,
    fc1_bias,
    fc2_weight,
    pair_source,
    pair_target,
    kept_order,
):
    images, own_tokens, width = tokens.shape
    length = sizes.shape[1]
    kept_total = kept_order.shape[1]
    devices_mp = lax.axis_size("mp")
    own_start = lax.axis_index("mp") * own_tokens
    head_size = D // HEADS
    base = tokens.astype(jnp.float32)
    normed = layer_norm(base, ln1_gain).astype(jnp.bfloat16)
    whole = lax.all_gather(normed, "mp", axis=1, tiled=True)
    local_width = qkv_weight.shape[2]
    columns = whole
    projected = jnp.einsum(
        "ind,cdf->cinf",
        columns,
        lax.all_gather(qkv_weight, "dp", axis=1, tiled=True),
        preferred_element_type=jnp.float32,
    ).astype(jnp.bfloat16)
    local_heads = local_width // head_size
    shaped = projected.reshape(3, images, length, local_heads, head_size)
    queries = shaped[0]
    keys_all = shaped[1]
    values_all = shaped[2]
    size_bias = jnp.log(sizes)[:, None, None, :]
    block = min(512, length)
    outputs = []
    for begin in range(0, length, block):
        scores = (
            jnp.einsum(
                "iqhe,ikhe->ihqk",
                queries[:, begin : begin + block],
                keys_all,
                preferred_element_type=jnp.float32,
            )
            / math.sqrt(head_size)
            + size_bias
        )
        weights = jax.nn.softmax(scores, axis=-1).astype(jnp.bfloat16)
        attended_block = jnp.einsum(
            "ihqk,ikhe->iqhe", weights, values_all, preferred_element_type=jnp.float32
        )
        outputs.append(attended_block.astype(jnp.bfloat16).reshape(images, block, local_width))
    attended = jnp.concatenate(outputs, axis=1)
    branch = jnp.einsum(
        "ind,de->ine",
        attended,
        lax.all_gather(proj_weight, "dp", axis=1, tiled=True),
        preferred_element_type=jnp.float32,
    )
    weighted = sizes[:, :, None] * branch
    own_sizes = lax.dynamic_slice_in_dim(sizes, own_start, own_tokens, 1)
    own_weighted = own_sizes[:, :, None] * base
    local_total = lax.dynamic_update_slice_in_dim(
        weighted,
        lax.dynamic_slice_in_dim(weighted, own_start, own_tokens, 1) + own_weighted,
        own_start,
        1,
    )
    merged_count = kept_total // devices_mp
    own_order = lax.dynamic_slice_in_dim(
        kept_order, lax.axis_index("mp") * merged_count, merged_count, 1
    )
    scattered = lax.psum_scatter(
        jnp.transpose(
            merge_rows(local_total, kept_order, pair_source, pair_target), (1, 0, 2)
        ).astype(jnp.bfloat16),
        "mp",
        scatter_dimension=0,
        tiled=True,
    ).astype(jnp.float32)
    numerator = jnp.transpose(scattered, (1, 0, 2))
    merged_size = merge_rows(sizes[:, :, None], own_order, pair_source, pair_target)
    merged = numerator / merged_size
    normed_two = layer_norm(merged, ln2_gain).astype(jnp.bfloat16)
    gathered = lax.all_gather(normed_two, "mp", axis=1, tiled=True)
    columns = gathered
    hidden_sum = jnp.einsum(
        "imd,df->imf",
        columns,
        lax.all_gather(fc1_weight, "dp", axis=0, tiled=True),
        preferred_element_type=jnp.float32,
    )
    hidden = jax.nn.gelu(hidden_sum + fc1_bias).astype(jnp.bfloat16)
    partial_out = jnp.einsum(
        "imf,fd->imd",
        hidden,
        lax.all_gather(fc2_weight, "dp", axis=1, tiled=True),
        preferred_element_type=jnp.float32,
    )
    mlp_part = lax.psum_scatter(
        partial_out.astype(jnp.bfloat16), "mp", scatter_dimension=1, tiled=True
    ).astype(jnp.float32)
    return (merged + mlp_part).astype(jnp.bfloat16)


def solution(mesh):
    return jax.shard_map(
        shards,
        mesh=mesh,
        in_specs=(
            P("dp", "mp", None),
            P("dp", None),
            P(),
            P(None, "dp", "mp"),
            P("mp", "dp"),
            P(),
            P("dp", "mp"),
            P("mp"),
            P("mp", "dp"),
            P("dp", None),
            P("dp", None),
            P("dp", None),
        ),
        out_specs=P("dp", "mp", None),
        check_vma=False,
    )
```

profile of v0, /device:TPU:1, one launch (start us, length us, event | category | flops | bytes accessed | tf_op | source)
XLA Modules:
  0.0 317.7 jit_solution(4380768634615341311)
XLA Ops:
  6.5 0.0 all-gather.6.cloned.1.call-start
  6.6 1.3 convert_reduce_fusion
  7.9 1.4 fusion.30
  9.3 2.2 fusion.32
  11.5 0.0 all-gather.6.cloned.1.call-update
  11.6 0.0 all-gather.8.cloned.1.call-start
  11.6 0.7 all-gather.8.cloned.1.call-update
  12.3 0.0 all-gather.12.cloned.1.call-start
  12.4 0.7 all-gather.12.cloned.1.call-update
  13.0 0.0 all-gather.14.cloned.1.call-start
  13.1 0.5 all-gather.14.cloned.1.call-update
  13.6 0.0 all-gather.10.cloned.1.call-start
  13.8 28.3 %all_gather.20 = bf16[320,1280]{0,1:T(8,128)(2,1)S(1)} all-gather(bf16[320,160]{0,1:T(8,128)(2,1)S(1)} %copy-done.2), channel_id=1, replica_groups=mesh['dp'=8,'mp'=4] {'dp'}, dimensions={1}, use_global_device_ids=true | all-gather | bytes 921600 | tf_op jit(solution)/shard_map/all_gather | solution.py:85
  42.1 0.1 compare_select_fusion.2
  42.2 0.6 gather_fusion.3
  42.8 1.4 gather_fusion.2
  44.2 0.2 fusion.56
  44.4 53.4 %all-gather.8.cloned.1.call-done = bf16[3,1280,320]{2,1,0:T(8,128)(2,1)} async-done(((bf16[3,160,320]{2,1,0:T(8,128)(2,1)}), bf16[3,1280,320]{2,1,0:T(8,128)(2,1)}) %all-gather.8.cloned.1.call-update) | async-done | bytes 2457616 | tf_op jit(solution)/shard_map/all_gather | solution.py:54
  97.8 5.4 %convert_bitcast_fusion = bf16[3,1,1024,320]{2,3,0,1:T(8,128)(2,1)S(1)} fusion(bf16[3,1280,320]{2,1,0:T(8,128)(2,1)} %all-gather.8.cloned.1.call-done, bf16[1,1024,1280]{2,1,0:T(8,128)(2,1)} %all-gather.6.cloned.1.call-done), kind=kOutput, calls=%fused_computation.38 | convolution fusion | flops 2517565440 | bytes 7045120 | tf_op jit(solution)/shard_map/ind,cdf->cinf/dot_general | solution.py:51
  103.2 0.2 fusion.78
  103.3 4.9 %fusion.80 = (f32[4,512]{1,0:T(4,128)S(1)}, f32[4,512,1024]{2,1,0:T(8,128)}) fusion(f32[1024]{0:T(1024)S(1)} %bitcast.179, bf16[1024,4,80]{0,2,1:T(8,128)(2,1)S(1)} %bitcast.170, bf16[1,1024,4,80]{1,3,2,0:T(8,128)(2,1)S(1)} %bitcast.168), kind=kOutput, calls=%fused_computation.120 | convolution fusion | flops 343933952 | bytes 9383936 | tf_op jit(solution)/shard_map/sub | solution.py:76
  108.2 4.9 %fusion.79 = (f32[4,512]{1,0:T(4,128)S(1)}, f32[4,512,1024]{2,1,0:T(8,128)}) fusion(f32[1024]{0:T(1024)S(1)} %bitcast.180, bf16[1024,4,80]{0,2,1:T(8,128)(2,1)S(1)} %bitcast.171, bf16[1,1024,4,80]{1,3,2,0:T(8,128)(2,1)S(1)} %bitcast.169), kind=kOutput, calls=%fused_computation.119 | convolution fusion | flops 343933952 | bytes 9383936 | tf_op jit(solution)/shard_map/sub | solution.py:76
  113.0 5.1 %fusion.37 = bf16[4,80,512]{2,1,0:T(8,128)(2,1)S(1)} fusion(bf16[1024,4,80]{0,2,1:T(8,128)(2,1)S(1)} %bitcast.166, f32[4,512,1024]{2,1,0:T(8,128)} %get-tuple-element.13, f32[4,512]{1,0:T(4,128)S(1)} %get-tuple-element.12), kind=kOutput, calls=%fused_computation.55 | convolution fusion | flops 339902464 | bytes 9379840 | tf_op jit(solution)/shard_map/ihqk,ikhe->iqhe/dot_general | solution.py:77
  118.1 0.8 copy-done.9
  118.9 1.7 fusion.36
  120.6 4.0 %convolution_multiply_fusion = f32[1024,1280]{1,0:T(8,128)} fusion(bf16[320,1280]{0,1:T(8,128)(2,1)S(1)} %all_gather.20, f32[1024]{0:T(1024)S(1)} %bitcast.165, bf16[1,512,320]{1,2,0:T(8,128)(2,1)S(1)} %bitcast.173, bf16[1,512,320]{1,2,0:T(8,128)(2,1)S(1)} %bitcast.172), kind=kOutput, calls=%fused_computation.24 | convolution fusion | flops 841482240 | bytes 6721536 | tf_op jit(solution)/shard_map/ind,de->ine/dot_general | solution.py:82
  124.6 1.4 constant_dynamic-slice_fusion.2
  126.0 1.3 fusion.35
  127.3 3.1 gather_fusion.1
  130.5 9.7 %gather_fusion = f32[1008,1280]{1,0:T(8,128)} fusion(f32[1024,1280]{1,0:T(8,128)} %fusion.35, s32[1024]{0:T(1024)S(1)} %pad_clamp_fusion.2), kind=kCustom, calls=%fused_computation | custom fusion | bytes 10325952 | tf_op jit(solution)/shard_map/jit(take_along_axis)/gather | solution.py:18
  140.1 5.1 %fusion.21 = bf16[1008,1,1280]{2,0,1:T(8,128)(2,1)S(1)} fusion(f32[1008,1280]{1,0:T(8,128)} %gather_fusion, pred[1008]{0:T(1024)(128)(4,1)S(1)} %compare_and_fusion, f32[16,1280]{1,0:T(8,128)S(1)} %gather_fusion.1, pred[16]{0:T(512)(128)(4,1)S(1)} %compare_and_fusion.1, s32[1008]{0:T(1024)S(1)} %bitcast.175, s32[16]{0:T(128)S(1)} %bitcast.185), kind=kOutput, calls=%fused_computation.33 | convolution fusion | flops 251633408 | bytes 7828480 | tf_op jit(solution)/shard_map/icr,ird->icd/dot_general | solution.py:21
  145.2 27.6 %fusion = bf16[256,1280]{1,0:T(8,128)(2,1)S(1)} fusion(bf16[1008,1,1280]{2,0,1:T(8,128)(2,1)S(1)} %fusion.21), kind=kCustom, calls=%all-reduce-scatter | all-reduce-scatter fusion | flops 1310721 | bytes 3236352
  172.8 4.4 %collective-permute-start = (bf16[12,1280]{1,0:T(8,128)(2,1)S(1)}, bf16[12,1280]{1,0:T(8,128)(2,1)S(1)}, u32[]{:S(2)}, u32[]{:S(2)}) collective-permute-start(bf16[12,1280]{1,0:T(8,128)(2,1)S(1)} %slice.36), channel_id=1, source_target_pairs={{0,1},{1,2},{2,3},{4,5},{5,6},{6,7},{8,9},{9,10},{10,11},{12,13},{... | collective-permute-start | bytes 92168
  177.2 0.6 dynamic-slice.10
  178.5 1.1 concatenate.4
  179.6 0.4 fusion.46
  180.0 0.5 multiply_reduce_fusion
  180.5 0.4 multiply_convert_fusion
  180.9 2.1 copy.14
  183.0 0.0 all-gather.12.cloned.1.call-done
  183.1 39.2 %all-gather.14.cloned.1.call-done = bf16[1280,1280]{0,1:T(8,128)(2,1)} async-done(((bf16[1280,160]{0,1:T(8,128)(2,1)}), bf16[1280,1280]{0,1:T(8,128)(2,1)}) %all-gather.14.cloned.1.call-update) | async-done | bytes 3276816 | tf_op jit(solution)/shard_map/all_gather | solution.py:125
  222.2 42.2 %all-gather.10.cloned.1.call-done = bf16[1,1008,1280]{2,0,1:T(2,128)(2,1)} async-done(((bf16[1,252,1280]{2,0,1:T(2,128)(2,1)}), bf16[1,1008,1280]{2,0,1:T(2,128)(2,1)}) %all-gather.10.cloned.1.call-update) | async-done | bytes 2580496 | tf_op jit(solution)/shard_map/all_gather | solution.py:113
  264.5 12.8 %fusion.20 = bf16[1,1008,1280]{2,1,0:T(8,128)(2,1)} fusion(bf16[1280,1280]{0,1:T(8,128)(2,1)} %all-gather.14.cloned.1.call-done, bf16[1280,1280]{1,0:T(8,128)(2,1)} %all-gather.12.cloned.1.call-done, bf16[1,1008,1280]{2,0,1:T(2,128)(2,1)} %all-gather.10.cloned.1.call-done, f32[1280]{0:T(1024)S(1)} %copy-done.7), kind=kOutput, calls=%fused_computation.32 | convolution fusion | flops 6620221440 | bytes 11719680 | tf_op jit(solution)/shard_map/imf,fd->imd/dot_general | solution.py:122
  277.3 26.0 %fusion.1 = bf16[256,1280]{1,0:T(8,128)(2,1)S(1)} fusion(bf16[1,1008,1280]{2,1,0:T(8,128)(2,1)} %fusion.20), kind=kCustom, calls=%all-reduce-scatter.1 | all-reduce-scatter fusion | flops 1310721 | bytes 3236352
  303.4 4.4 %collective-permute-start.1 = (bf16[12,1280]{1,0:T(8,128)(2,1)S(1)}, bf16[12,1280]{1,0:T(8,128)(2,1)S(1)}, u32[]{:S(2)}, u32[]{:S(2)}) collective-permute-start(bf16[12,1280]{1,0:T(8,128)(2,1)S(1)} %slice.37), channel_id=1, source_target_pairs={{0,1},{1,2},{2,3},{4,5},{5,6},{6,7},{8,9},{9,10},{10,11},{12,13},{... | collective-permute-start | bytes 92168
  307.8 1.1 collective-permute-done.1
  308.9 1.0 concatenate.5
  309.9 1.3 add_convert_fusion.1
  (38 shorter events, 0.2 us)
Async XLA Ops:
  6.5 7.1 %copy-start.8 = (s32[1,16]{1,0:T(1,128)S(1)}, s32[1,16]{1,0:T(1,128)}, u32[]{:S(2)}) copy-start(s32[1,16]{1,0:T(1,128)} %param.21) | copy-start | bytes 196
  6.5 7.2 %copy-start = (f32[1,1024]{1,0:T(1,128)S(1)}, f32[1,1024]{1,0:T(1,128)}, u32[]{:S(2)}) copy-start(f32[1,1024]{1,0:T(1,128)} %param.13) | copy-start | bytes 12292
  6.5 7.2 %copy-start.2 = (bf16[320,160]{0,1:T(8,128)(2,1)S(1)}, bf16[320,160]{0,1:T(8,128)(2,1)}, u32[]{:S(2)}) copy-start(bf16[320,160]{0,1:T(8,128)(2,1)} %param.16) | copy-start | bytes 307204
  6.5 35.5 %copy-start.3 = (s32[1,1008]{1,0:T(1,128)S(1)}, s32[1,1008]{1,0:T(1,128)}, u32[]{:S(2)}) copy-start(s32[1,1008]{1,0:T(1,128)} %param.23) | copy-start | bytes 12100
  6.5 37.8 %all-gather.6.cloned.1.call-start = ((), (), s32[]{:S(2)}) async-start(), calls=%async_computation | async-start | bytes 3276800 | tf_op jit(solution)/shard_map/all_gather | solution.py:48
  7.9 36.3 %copy-start.5 = (s32[1,16]{1,0:T(1,128)S(1)}, s32[1,16]{1,0:T(1,128)}, u32[]{:S(2)}) copy-start(s32[1,16]{1,0:T(1,128)} %param.22) | copy-start | bytes 196
  11.6 86.2 %all-gather.8.cloned.1.call-start = ((), (), s32[]{:S(2)}) async-start(), calls=%async_computation.1 | async-start | bytes 3317760 | tf_op jit(solution)/shard_map/all_gather | solution.py:54
  12.3 170.7 %all-gather.12.cloned.1.call-start = ((), (), s32[]{:S(2)}) async-start(), calls=%async_computation.3 | async-start | bytes 3686400 | tf_op jit(solution)/shard_map/all_gather | solution.py:118
  13.0 209.2 %all-gather.14.cloned.1.call-start = ((), (), s32[]{:S(2)}) async-start(), calls=%async_computation.4 | async-start | bytes 3686400 | tf_op jit(solution)/shard_map/all_gather | solution.py:125
  13.6 250.8 %all-gather.10.cloned.1.call-start = ((), (), s32[]{:S(2)}) async-start(), calls=%async_computation.2 | async-start | bytes 6451200 | tf_op jit(solution)/shard_map/all_gather | solution.py:113
  113.0 5.9 %copy-start.9 = (f32[4,512,1024]{2,1,0:T(8,128)S(1)}, f32[4,512,1024]{2,1,0:T(8,128)}, u32[]{:S(2)}) copy-start(f32[4,512,1024]{2,1,0:T(8,128)} %get-tuple-element.11) | copy-start | bytes 25165828
  120.6 5.4 %copy-start.1 = (bf16[1,256,1280]{2,1,0:T(8,128)(2,1)S(1)}, bf16[1,256,1280]{2,1,0:T(8,128)(2,1)}, u32[]{:S(2)}) copy-start(bf16[1,256,1280]{2,1,0:T(8,128)(2,1)} %param.12) | copy-start | bytes 1966084
  145.2 32.0 %copy-start.6 = (u32[32]{0:T(128)S(1)}, u32[32]{0:T(128)}, u32[]{:S(2)}) copy-start(u32[32]{0:T(128)} %constant.99) | copy-start | bytes 388
  145.2 35.3 %copy-start.4 = (f32[1280]{0:T(1024)S(1)}, f32[1280]{0:T(1024)}, u32[]{:S(2)}) copy-start(f32[1280]{0:T(1024)} %param.17) | copy-start | bytes 15364
  172.8 5.7 %collective-permute-start = (bf16[12,1280]{1,0:T(8,128)(2,1)S(1)}, bf16[12,1280]{1,0:T(8,128)(2,1)S(1)}, u32[]{:S(2)}, u32[]{:S(2)}) collective-permute-start(bf16[12,1280]{1,0:T(8,128)(2,1)S(1)} %slice.36), channel_id=1, source_target_pairs={{0,1},{1,2},{2,3},{4,5},{5,6},{6,7},{8,9},{9,10},{10,11},{12,13},{... | collective-permute-start | bytes 92168
  179.6 84.9 %copy-start.7 = (f32[1280]{0:T(1024)S(1)}, f32[1280]{0:T(1024)}, u32[]{:S(2)}) copy-start(f32[1280]{0:T(1024)} %param.19) | copy-start | bytes 15364
  303.4 5.5 %collective-permute-start.1 = (bf16[12,1280]{1,0:T(8,128)(2,1)S(1)}, bf16[12,1280]{1,0:T(8,128)(2,1)S(1)}, u32[]{:S(2)}, u32[]{:S(2)}) collective-permute-start(bf16[12,1280]{1,0:T(8,128)(2,1)S(1)} %slice.37), channel_id=1, source_target_pairs={{0,1},{1,2},{2,3},{4,5},{5,6},{6,7},{8,9},{9,10},{10,11},{12,13},{... | collective-permute-start | bytes 92168
Sparse Core Ops, SparseCore 0:
  11.7 27.9 all-gather.5
  41.9 55.8 all-gather.7
  100.0 59.9 all-gather.11
  162.0 60.1 all-gather.13
  223.6 40.7 all-gather.9
where the time goes:
time: 318 us
  waiting for transfers between devices  138 us (43%)
  blocking collectives  81.9 us (26%)
  matrix products  44 us (14%)
  local copies, waits for them, and re-layouts  22 us (7%)
  between operations  14.1 us (4%)
  starting transfers between devices  8.96 us (3%)
  other arithmetic  8.93 us (3%)
    unnamed x2, blocking collectives  53.6 us
    all_gather x1, waiting for transfers between devices, shards(): lax.all_gather(qkv_weight, 'dp', axis=1, tiled=True)  53.4 us
    all_gather x1, waiting for transfers between devices, shards(): gathered = lax.all_gather(normed_two, 'mp', axis=1, tiled=True)  42.2 us
    all_gather x1, waiting for transfers between devices, shards(): lax.all_gather(fc2_weight, 'dp', axis=1, tiled=True)  39.2 us
    all_gather x1, blocking collectives, shards(): lax.all_gather(proj_weight, 'dp', axis=1, tiled=True)  28.3 us
    dot_general x1, matrix products, shards(): jnp.einsum('imf,fd->imd', hidden, lax.all_gather(fc2_weight, 'dp', axis=1...  12.8 us
    gather x2, local copies, waits for them, and re-layouts, merge_rows(): kept_rows = jnp.take_along_axis(total, order_rows[:, :, None], axis=1)  11 us
    sub x2, matrix products, shards(): weights = jax.nn.softmax(scores, axis=-1).astype(jnp.bfloat16)  9.7 us
  transfers between devices with their start and end apart: 7, of which 4 were waited for; matrix products, arithmetic and copies ran while one was open for 26% of the time, Pallas kernels for 0%

commit v1 on v0

--- a/solution.py
+++ b/solution.py
@@ -6,6 +6,27 @@
 
 D = 1280
 HEADS = 16
+
+
+def notes_serve(field, join_dim, work_x, at_axis):
+    shard_axis = "dp"
+    base_arr = lax.axis_size(shard_axis)
+    arr_now = lax.axis_index(shard_axis)
+    b_now, parts_out, f_next = (base_arr, arr_now, field.shape[join_dim])
+    crops = []
+    for at in range(b_now):
+        t1 = (
+            lax.ppermute(
+                field, shard_axis, perm=[(src_i, (src_i + 1) % b_now) for src_i in range(b_now)]
+            )
+            if at + 1 < b_now
+            else field
+        )
+        odd = work_x(field, (parts_out - at) % b_now * f_next)
+        crops.append(odd)
+        field = t1
+    row_out = jnp.concatenate(crops[::-1], axis=at_axis)
+    return jnp.roll(row_out, (parts_out + 1) * crops[0].shape[at_axis], axis=at_axis)
 
 
 def layer_norm(values, gain):
@@ -119,11 +140,13 @@
         preferred_element_type=jnp.float32,
     )
     hidden = jax.nn.gelu(hidden_sum + fc1_bias).astype(jnp.bfloat16)
-    partial_out = jnp.einsum(
-        "imf,fd->imd",
-        hidden,
-        lax.all_gather(fc2_weight, "dp", axis=1, tiled=True),
-        preferred_element_type=jnp.float32,
+    partial_out = notes_serve(
+        fc2_weight,
+        1,
+        lambda own_block, at: jnp.einsum(
+            "imf,fd->imd", hidden, own_block, preferred_element_type=jnp.float32
+        ),
+        2,
     )
     mlp_part = lax.psum_scatter(
         partial_out.astype(jnp.bfloat16), "mp", scatter_dimension=1, tiled=True

time: 318 us -> 339 us (1.066)
  local copies, waits for them, and re-layouts: 22 us -> 38.6 us
  matrix products: 44 us -> 51 us
  waiting for transfers between devices: 138 us -> 132 us
    ppermute x0 -> x7, waiting for transfers between devices: none -> 75.3 us  [notes_serve(): lax.ppermute(field, shard_axis, perm=[(src_i, (src_i + 1) % b_now) for sr...]
    all_gather x1, waiting for transfers between devices: 42.2 us -> 0.01 us  [shards(): gathered = lax.all_gather(normed_two, 'mp', axis=1, tiled=True)]
    all_gather x1 -> x0, waiting for transfers between devices: 39.2 us -> none  [shards(): lax.all_gather(fc2_weight, 'dp', axis=1, tiled=True)]
    concatenate x0 -> x1, local copies, waits for them, and re-layouts: none -> 10.4 us  [notes_serve(): jnp.roll(row_out, (parts_out + 1) * crops[0].shape[at_axis], axis=at_axis)]
    dot_general x1 -> x9, matrix products: 12.8 us -> 19.9 us  [the longest x8 12.1 us: shards(): jnp.einsum('imf,fd->imd', hidden, own_block, preferred_element_type=jnp.f...]
  transfers between devices with their start and end apart: 7 -> 13, of which waited for: 4 -> 8; matrix products, arithmetic and copies ran while one was open for 26% -> 29% of each run, Pallas kernels for 0% -> 0%
where the time goes in v1:
time: 339 us; the launch traced here: 338 us
  waiting for transfers between devices  132 us (39%)
  blocking collectives  84.2 us (25%)
  matrix products  51 us (15%)
  local copies, waits for them, and re-layouts  38.6 us (11%)
  between operations  14.2 us (4%)
  starting transfers between devices  9 us (3%)
  other arithmetic  8.91 us (3%)
    ppermute x7, waiting for transfers between devices, notes_serve(): lax.ppermute(field, shard_axis, perm=[(src_i, (src_i + 1) % b_now) for sr...  75.3 us
    unnamed x2, blocking collectives  55.9 us
    all_gather x1, waiting for transfers between devices, shards(): lax.all_gather(qkv_weight, 'dp', axis=1, tiled=True)  54 us
    all_gather x1, blocking collectives, shards(): lax.all_gather(proj_weight, 'dp', axis=1, tiled=True)  28.3 us
    dot_general x8, matrix products, shards(): jnp.einsum('imf,fd->imd', hidden, own_block, preferred_element_type=jnp.f...  12.1 us
    gather x2, local copies, waits for them, and re-layouts, merge_rows(): kept_rows = jnp.take_along_axis(total, order_rows[:, :, None], axis=1)  11.1 us
    concatenate x1, local copies, waits for them, and re-layouts, notes_serve(): jnp.roll(row_out, (parts_out + 1) * crops[0].shape[at_axis], axis=at_axis)  10.4 us
    sub x2, matrix products, shards(): weights = jax.nn.softmax(scores, axis=-1).astype(jnp.bfloat16)  9.67 us
  transfers between devices with their start and end apart: 13, of which 8 were waited for; matrix products, arithmetic and copies ran while one was open for 29% of the time, Pallas kernels for 0%

profile of v1, /device:TPU:1, one launch (start us, length us, event | category | flops | bytes accessed | tf_op | source)
XLA Modules:
  0.0 337.6 jit_solution(4954327375171128891)
XLA Ops:
  6.6 1.3 convert_reduce_fusion
  7.9 1.4 fusion.29
  9.3 2.2 fusion.31
  11.6 0.7 all-gather.7.cloned.1.call-update
  12.4 0.7 all-gather.11.cloned.1.call-update
  13.2 28.3 %all_gather.17 = bf16[320,1280]{0,1:T(8,128)(2,1)S(1)} all-gather(bf16[320,160]{0,1:T(8,128)(2,1)S(1)} %copy-done.2), channel_id=1, replica_groups=mesh['dp'=8,'mp'=4] {'dp'}, dimensions={1}, use_global_device_ids=true | all-gather | bytes 921600 | tf_op jit(solution)/shard_map/all_gather | solution.py:106
  41.6 0.6 gather_fusion.3
  42.2 1.4 gather_fusion.2
  43.8 54.0 %all-gather.7.cloned.1.call-done = bf16[3,1280,320]{2,1,0:T(8,128)(2,1)} async-done(((bf16[3,160,320]{2,1,0:T(8,128)(2,1)}), bf16[3,1280,320]{2,1,0:T(8,128)(2,1)}) %all-gather.7.cloned.1.call-update) | async-done | bytes 2457616 | tf_op jit(solution)/shard_map/all_gather | solution.py:75
  97.8 5.4 %convert_bitcast_fusion = bf16[3,1,1024,320]{2,3,0,1:T(8,128)(2,1)S(1)} fusion(bf16[3,1280,320]{2,1,0:T(8,128)(2,1)} %all-gather.7.cloned.1.call-done, bf16[1,1024,1280]{2,1,0:T(8,128)(2,1)} %all-gather.5.cloned.1.call-done), kind=kOutput, calls=%fused_computation.37 | convolution fusion | flops 2517565440 | bytes 7045120 | tf_op jit(solution)/shard_map/ind,cdf->cinf/dot_general | solution.py:72
  103.3 4.8 %fusion.73 = (f32[4,512]{1,0:T(4,128)S(1)}, f32[4,512,1024]{2,1,0:T(8,128)}) fusion(f32[1024]{0:T(1024)S(1)} %bitcast.206, bf16[1024,4,80]{0,2,1:T(8,128)(2,1)S(1)} %bitcast.197, bf16[1,1024,4,80]{1,3,2,0:T(8,128)(2,1)S(1)} %bitcast.195), kind=kOutput, calls=%fused_computation.123 | convolution fusion | flops 343933952 | bytes 9383936 | tf_op jit(solution)/shard_map/sub | solution.py:97
  108.1 4.8 %fusion.72 = (f32[4,512]{1,0:T(4,128)S(1)}, f32[4,512,1024]{2,1,0:T(8,128)}) fusion(f32[1024]{0:T(1024)S(1)} %bitcast.207, bf16[1024,4,80]{0,2,1:T(8,128)(2,1)S(1)} %bitcast.198, bf16[1,1024,4,80]{1,3,2,0:T(8,128)(2,1)S(1)} %bitcast.196), kind=kOutput, calls=%fused_computation.122 | convolution fusion | flops 343933952 | bytes 9383936 | tf_op jit(solution)/shard_map/sub | solution.py:97
  113.0 5.0 %fusion.36 = bf16[4,80,512]{2,1,0:T(8,128)(2,1)S(1)} fusion(bf16[1024,4,80]{0,2,1:T(8,128)(2,1)S(1)} %bitcast.193, f32[4,512,1024]{2,1,0:T(8,128)} %get-tuple-element.13, f32[4,512]{1,0:T(4,128)S(1)} %get-tuple-element.12), kind=kOutput, calls=%fused_computation.62 | convolution fusion | flops 339902464 | bytes 9379840 | tf_op jit(solution)/shard_map/ihqk,ikhe->iqhe/dot_general | solution.py:98
  118.0 0.8 copy-done.16
  118.9 1.7 fusion.35
  120.6 4.0 %convolution_multiply_fusion = f32[1024,1280]{1,0:T(8,128)} fusion(bf16[320,1280]{0,1:T(8,128)(2,1)S(1)} %all_gather.17, f32[1024]{0:T(1024)S(1)} %bitcast.192, bf16[1,512,320]{1,2,0:T(8,128)(2,1)S(1)} %bitcast.200, bf16[1,512,320]{1,2,0:T(8,128)(2,1)S(1)} %bitcast.199), kind=kOutput, calls=%fused_computation.25 | convolution fusion | flops 841482240 | bytes 6721536 | tf_op jit(solution)/shard_map/ind,de->ine/dot_general | solution.py:103
  124.6 1.5 constant_dynamic-slice_fusion.2
  126.1 1.3 fusion.34
  127.4 3.1 gather_fusion.1
  130.5 9.7 %gather_fusion = f32[1008,1280]{1,0:T(8,128)} fusion(f32[1024,1280]{1,0:T(8,128)} %fusion.34, s32[1024]{0:T(1024)S(1)} %pad_clamp_fusion.2), kind=kCustom, calls=%fused_computation | custom fusion | bytes 10325952 | tf_op jit(solution)/shard_map/jit(take_along_axis)/gather | solution.py:39
  140.2 5.1 %fusion.20 = bf16[1008,1,1280]{2,0,1:T(8,128)(2,1)S(1)} fusion(f32[1008,1280]{1,0:T(8,128)} %gather_fusion, pred[1008]{0:T(1024)(128)(4,1)S(1)} %compare_and_fusion, f32[16,1280]{1,0:T(8,128)S(1)} %gather_fusion.1, pred[16]{0:T(512)(128)(4,1)S(1)} %compare_and_fusion.1, s32[1008]{0:T(1024)S(1)} %bitcast.202, s32[16]{0:T(128)S(1)} %bitcast.212), kind=kOutput, calls=%fused_computation.32 | convolution fusion | flops 251633408 | bytes 7828480 | tf_op jit(solution)/shard_map/icr,ird->icd/dot_general | solution.py:42
  145.3 27.6 %fusion = bf16[256,1280]{1,0:T(8,128)(2,1)S(1)} fusion(bf16[1008,1,1280]{2,0,1:T(8,128)(2,1)S(1)} %fusion.20), kind=kCustom, calls=%all-reduce-scatter | all-reduce-scatter fusion | flops 1310721 | bytes 3236352
  172.9 4.4 %collective-permute-start.7 = (bf16[12,1280]{1,0:T(8,128)(2,1)S(1)}, bf16[12,1280]{1,0:T(8,128)(2,1)S(1)}, u32[]{:S(2)}, u32[]{:S(2)}) collective-permute-start(bf16[12,1280]{1,0:T(8,128)(2,1)S(1)} %slice.36), channel_id=1, source_target_pairs={{0,1},{1,2},{2,3},{4,5},{5,6},{6,7},{8,9},{9,10},{10,11},{12,13},{... | collective-permute-start | bytes 92168
  178.5 1.1 concatenate.11
  181.0 2.1 copy.33
  183.2 12.6 %collective-permute-done = bf16[1280,160]{0,1:T(8,128)(2,1)S(1)} collective-permute-done((bf16[1280,160]{0,1:T(8,128)(2,1)S(1)}, bf16[1280,160]{0,1:T(8,128)(2,1)S(1)}, u32[]{:S(2)}, u32[]{:S(2)}) %collective-permute-start) | collective-permute-done | bytes 409632 | tf_op jit(solution)/shard_map/ppermute | solution.py:19
  195.8 14.0 %collective-permute-done.1 = bf16[1280,160]{0,1:T(8,128)(2,1)S(1)} collective-permute-done((bf16[1280,160]{0,1:T(8,128)(2,1)S(1)}, bf16[1280,160]{0,1:T(8,128)(2,1)S(1)}, u32[]{:S(2)}, u32[]{:S(2)}) %collective-permute-start.1) | collective-permute-done | bytes 409632 | tf_op jit(solution)/shard_map/ppermute | solution.py:19
  209.9 13.3 %collective-permute-done.2 = bf16[1280,160]{0,1:T(8,128)(2,1)S(1)} collective-permute-done((bf16[1280,160]{0,1:T(8,128)(2,1)S(1)}, bf16[1280,160]{0,1:T(8,128)(2,1)S(1)}, u32[]{:S(2)}, u32[]{:S(2)}) %collective-permute-start.2) | collective-permute-done | bytes 409632 | tf_op jit(solution)/shard_map/ppermute | solution.py:19
  223.2 12.5 %collective-permute-done.3 = bf16[1280,160]{0,1:T(8,128)(2,1)S(1)} collective-permute-done((bf16[1280,160]{0,1:T(8,128)(2,1)S(1)}, bf16[1280,160]{0,1:T(8,128)(2,1)S(1)}, u32[]{:S(2)}, u32[]{:S(2)}) %collective-permute-start.3) | collective-permute-done | bytes 409632 | tf_op jit(solution)/shard_map/ppermute | solution.py:19
  235.7 11.7 %collective-permute-done.4 = bf16[1280,160]{0,1:T(8,128)(2,1)} collective-permute-done((bf16[1280,160]{0,1:T(8,128)(2,1)S(1)}, bf16[1280,160]{0,1:T(8,128)(2,1)}, u32[]{:S(2)}, u32[]{:S(2)}) %collective-permute-start.4) | collective-permute-done | bytes 409632 | tf_op jit(solution)/shard_map/ppermute | solution.py:19
  247.4 11.1 %collective-permute-done.5 = bf16[1280,160]{0,1:T(8,128)(2,1)} collective-permute-done((bf16[1280,160]{0,1:T(8,128)(2,1)}, bf16[1280,160]{0,1:T(8,128)(2,1)}, u32[]{:S(2)}, u32[]{:S(2)}) %collective-permute-start.5) | collective-permute-done | bytes 409632 | tf_op jit(solution)/shard_map/ppermute | solution.py:19
  258.5 7.8 %fusion.13 = bf16[1008,1280]{1,0:T(8,128)(2,1)S(1)} fusion(bf16[1280,1280]{1,0:T(8,128)(2,1)} %all-gather.11.cloned.1.call-done, bf16[1,1008,1280]{2,0,1:T(2,128)(2,1)} %all-gather.9.cloned.1.call-done, f32[1280]{0:T(1024)S(1)} %copy-done.14), kind=kOutput, calls=%fused_computation.22 | convolution fusion | flops 3315916800 | bytes 8442880 | tf_op jit(solution)/shard_map/imd,df->imf/dot_general | solution.py:136
  266.3 0.8 convolution_bitcast_fusion
  267.2 1.8 convolution_bitcast_fusion.6
  269.0 1.8 convolution_bitcast_fusion.5
  270.9 0.8 convolution_bitcast_fusion.4
  271.9 0.8 convolution_bitcast_fusion.3
  272.9 1.6 convolution_bitcast_fusion.2
  274.5 1.6 convolution_bitcast_fusion.1
  276.2 2.6 convolution_bitcast_fusion.7
  278.8 10.4 %concatenate.10 = bf16[1,1008,2560]{2,1,0:T(8,128)(2,1)} concatenate(bf16[1,1008,160]{2,1,0:T(8,128)(2,1)} %convolution_bitcast_fusion.7, bf16[1,1008,160]{2,1,0:T(8,128)(2,1)S(1)} %convolution_bitcast_fusion.6, bf16[1,1008,160]{2,1,0:T(8,128)(2,1)S(1)} %convolution_bitcast_fusion.5, bf16[1,1008,160]{2,1,0:T(8,128)(2,1)S(1)} %convolution_bitcast_fusion.4, ...), dimensions={2} | concatenate | bytes 10321920 | tf_op jit(solution)/shard_map/jit(_roll_dynamic)/concatenate | solution.py:29
  289.2 3.0 dynamic-slice_convert_fusion
  292.2 28.4 %fusion.1 = bf16[256,1280]{1,0:T(8,128)(2,1)} fusion(bf16[1,1008,1280]{2,1,0:T(8,128)(2,1)S(1)} %dynamic-slice_convert_fusion), kind=kCustom, calls=%all-reduce-scatter.1 | all-reduce-scatter fusion | flops 1310721 | bytes 3236352
  320.6 0.8 slice.37
  321.4 4.4 %collective-permute-start.8 = (bf16[12,1280]{1,0:T(8,128)(2,1)S(1)}, bf16[12,1280]{1,0:T(8,128)(2,1)S(1)}, u32[]{:S(2)}, u32[]{:S(2)}) collective-permute-start(bf16[12,1280]{1,0:T(8,128)(2,1)S(1)} %slice.37), channel_id=1, source_target_pairs={{0,1},{1,2},{2,3},{4,5},{5,6},{6,7},{8,9},{9,10},{10,11},{12,13},{... | collective-permute-start | bytes 92168
  325.8 1.1 collective-permute-done.8
  326.8 3.0 concatenate.12
  329.9 1.3 add_convert_fusion.1
  (73 shorter events, 3.1 us)
Async XLA Ops:
  6.5 6.6 %copy-start.15 = (s32[1,16]{1,0:T(1,128)S(1)}, s32[1,16]{1,0:T(1,128)}, u32[]{:S(2)}) copy-start(s32[1,16]{1,0:T(1,128)} %param.21) | copy-start | bytes 196
  6.5 6.6 %copy-start = (f32[1,1024]{1,0:T(1,128)S(1)}, f32[1,1024]{1,0:T(1,128)}, u32[]{:S(2)}) copy-start(f32[1,1024]{1,0:T(1,128)} %param.13) | copy-start | bytes 12292
  6.5 6.6 %copy-start.2 = (bf16[320,160]{0,1:T(8,128)(2,1)S(1)}, bf16[320,160]{0,1:T(8,128)(2,1)}, u32[]{:S(2)}) copy-start(bf16[320,160]{0,1:T(8,128)(2,1)} %param.16) | copy-start | bytes 307204
  6.5 34.9 %copy-start.3 = (s32[1,1008]{1,0:T(1,128)S(1)}, s32[1,1008]{1,0:T(1,128)}, u32[]{:S(2)}) copy-start(s32[1,1008]{1,0:T(1,128)} %param.23) | copy-start | bytes 12100
  6.5 37.3 %all-gather.5.cloned.1.call-start = ((), (), s32[]{:S(2)}) async-start(), calls=%async_computation | async-start | bytes 3276800 | tf_op jit(solution)/shard_map/all_gather | solution.py:69
  9.3 34.3 %copy-start.5 = (s32[1,16]{1,0:T(1,128)S(1)}, s32[1,16]{1,0:T(1,128)}, u32[]{:S(2)}) copy-start(s32[1,16]{1,0:T(1,128)} %param.22) | copy-start | bytes 196
  11.6 86.2 %all-gather.7.cloned.1.call-start = ((), (), s32[]{:S(2)}) async-start(), calls=%async_computation.1 | async-start | bytes 3317760 | tf_op jit(solution)/shard_map/all_gather | solution.py:75
  12.3 246.1 %all-gather.11.cloned.1.call-start = ((), (), s32[]{:S(2)}) async-start(), calls=%async_computation.3 | async-start | bytes 3686400 | tf_op jit(solution)/shard_map/all_gather | solution.py:139
  13.1 245.4 %all-gather.9.cloned.1.call-start = ((), (), s32[]{:S(2)}) async-start(), calls=%async_computation.2 | async-start | bytes 6451200 | tf_op jit(solution)/shard_map/all_gather | solution.py:134
  113.0 5.9 %copy-start.16 = (f32[4,512,1024]{2,1,0:T(8,128)S(1)}, f32[4,512,1024]{2,1,0:T(8,128)}, u32[]{:S(2)}) copy-start(f32[4,512,1024]{2,1,0:T(8,128)} %get-tuple-element.11) | copy-start | bytes 25165828
  124.6 1.5 copy-start.1
  145.3 32.0 %copy-start.6 = (u32[32]{0:T(128)S(1)}, u32[32]{0:T(128)}, u32[]{:S(2)}) copy-start(u32[32]{0:T(128)} %constant.126) | copy-start | bytes 388
  145.3 35.3 %copy-start.4 = (f32[1280]{0:T(1024)S(1)}, f32[1280]{0:T(1024)}, u32[]{:S(2)}) copy-start(f32[1280]{0:T(1024)} %param.17) | copy-start | bytes 15364
  172.9 5.7 %collective-permute-start.7 = (bf16[12,1280]{1,0:T(8,128)(2,1)S(1)}, bf16[12,1280]{1,0:T(8,128)(2,1)S(1)}, u32[]{:S(2)}, u32[]{:S(2)}) collective-permute-start(bf16[12,1280]{1,0:T(8,128)(2,1)S(1)} %slice.36), channel_id=1, source_target_pairs={{0,1},{1,2},{2,3},{4,5},{5,6},{6,7},{8,9},{9,10},{10,11},{12,13},{... | collective-permute-start | bytes 92168
  180.1 3.1 copy-start.7
  180.1 78.4 %copy-start.14 = (f32[1280]{0:T(1024)S(1)}, f32[1280]{0:T(1024)}, u32[]{:S(2)}) copy-start(f32[1280]{0:T(1024)} %param.19) | copy-start | bytes 15364
  183.1 12.7 %collective-permute-start = (bf16[1280,160]{0,1:T(8,128)(2,1)S(1)}, bf16[1280,160]{0,1:T(8,128)(2,1)S(1)}, u32[]{:S(2)}, u32[]{:S(2)}) collective-permute-start(bf16[1280,160]{0,1:T(8,128)(2,1)S(1)} %copy-done.7), channel_id=1, source_target_pairs={{0,4},{4,8},{8,12},{12,16},{16,20},{20,24},{24,28},{28,0},{1,5},{5... | collective-permute-start | bytes 1228808 | tf_op jit(solution)/shard_map/ppermute | solution.py:19
  195.8 62.6 %copy-start.8 = (bf16[1280,160]{0,1:T(8,128)(2,1)}, bf16[1280,160]{0,1:T(8,128)(2,1)S(1)}, u32[]{:S(2)}) copy-start(bf16[1280,160]{0,1:T(8,128)(2,1)S(1)} %collective-permute-done) | copy-start | bytes 1228804
  195.8 14.0 %collective-permute-start.1 = (bf16[1280,160]{0,1:T(8,128)(2,1)S(1)}, bf16[1280,160]{0,1:T(8,128)(2,1)S(1)}, u32[]{:S(2)}, u32[]{:S(2)}) collective-permute-start(bf16[1280,160]{0,1:T(8,128)(2,1)S(1)} %collective-permute-done), channel_id=1, source_target_pairs={{0,4},{4,8},{8,12},{12,16},{16,20},{20,24},{24,28},{28,0},{1,5},{5... | collective-permute-start | bytes 1228808 | tf_op jit(solution)/shard_map/ppermute | solution.py:19
  209.9 56.5 %copy-start.10 = (bf16[1280,160]{0,1:T(8,128)(2,1)}, bf16[1280,160]{0,1:T(8,128)(2,1)S(1)}, u32[]{:S(2)}) copy-start(bf16[1280,160]{0,1:T(8,128)(2,1)S(1)} %collective-permute-done.1) | copy-start | bytes 1228804
  209.9 13.3 %collective-permute-start.2 = (bf16[1280,160]{0,1:T(8,128)(2,1)S(1)}, bf16[1280,160]{0,1:T(8,128)(2,1)S(1)}, u32[]{:S(2)}, u32[]{:S(2)}) collective-permute-start(bf16[1280,160]{0,1:T(8,128)(2,1)S(1)} %collective-permute-done.1), channel_id=1, source_target_pairs={{0,4},{4,8},{8,12},{12,16},{16,20},{20,24},{24,28},{28,0},{1,5},{5... | collective-permute-start | bytes 1228808 | tf_op jit(solution)/shard_map/ppermute | solution.py:19
  223.2 43.1 %copy-start.12 = (bf16[1280,160]{0,1:T(8,128)(2,1)}, bf16[1280,160]{0,1:T(8,128)(2,1)S(1)}, u32[]{:S(2)}) copy-start(bf16[1280,160]{0,1:T(8,128)(2,1)S(1)} %collective-permute-done.2) | copy-start | bytes 1228804
  223.2 12.5 %collective-permute-start.3 = (bf16[1280,160]{0,1:T(8,128)(2,1)S(1)}, bf16[1280,160]{0,1:T(8,128)(2,1)S(1)}, u32[]{:S(2)}, u32[]{:S(2)}) collective-permute-start(bf16[1280,160]{0,1:T(8,128)(2,1)S(1)} %collective-permute-done.2), channel_id=1, source_target_pairs={{0,4},{4,8},{8,12},{12,16},{16,20},{20,24},{24,28},{28,0},{1,5},{5... | collective-permute-start | bytes 1228808 | tf_op jit(solution)/shard_map/ppermute | solution.py:19
  235.7 11.7 %collective-permute-start.4 = (bf16[1280,160]{0,1:T(8,128)(2,1)S(1)}, bf16[1280,160]{0,1:T(8,128)(2,1)}, u32[]{:S(2)}, u32[]{:S(2)}) collective-permute-start(bf16[1280,160]{0,1:T(8,128)(2,1)S(1)} %collective-permute-done.3), channel_id=1, source_target_pairs={{0,4},{4,8},{8,12},{12,16},{16,20},{20,24},{24,28},{28,0},{1,5},{5... | collective-permute-start | bytes 1228808 | tf_op jit(solution)/shard_map/ppermute | solution.py:19
  247.4 11.1 %collective-permute-start.5 = (bf16[1280,160]{0,1:T(8,128)(2,1)}, bf16[1280,160]{0,1:T(8,128)(2,1)}, u32[]{:S(2)}, u32[]{:S(2)}) collective-permute-start(bf16[1280,160]{0,1:T(8,128)(2,1)} %collective-permute-done.4), channel_id=1, source_target_pairs={{0,4},{4,8},{8,12},{12,16},{16,20},{20,24},{24,28},{28,0},{1,5},{5... | collective-permute-start | bytes 1228808 | tf_op jit(solution)/shard_map/ppermute | solution.py:19
  258.5 17.7 %collective-permute-start.6 = (bf16[1280,160]{0,1:T(8,128)(2,1)}, bf16[1280,160]{0,1:T(8,128)(2,1)}, u32[]{:S(2)}, u32[]{:S(2)}) collective-permute-start(bf16[1280,160]{0,1:T(8,128)(2,1)} %collective-permute-done.5), channel_id=1, source_target_pairs={{0,4},{4,8},{8,12},{12,16},{16,20},{20,24},{24,28},{28,0},{1,5},{5... | collective-permute-start | bytes 1228808 | tf_op jit(solution)/shard_map/ppermute | solution.py:19
  270.9 1.0 copy-start.13
  271.9 1.0 copy-start.11
  272.9 1.6 copy-start.9
  321.4 5.5 %collective-permute-start.8 = (bf16[12,1280]{1,0:T(8,128)(2,1)S(1)}, bf16[12,1280]{1,0:T(8,128)(2,1)S(1)}, u32[]{:S(2)}, u32[]{:S(2)}) collective-permute-start(bf16[12,1280]{1,0:T(8,128)(2,1)S(1)} %slice.37), channel_id=1, source_target_pairs={{0,1},{1,2},{2,3},{4,5},{5,6},{6,7},{8,9},{9,10},{10,11},{12,13},{... | collective-permute-start | bytes 92168
Sparse Core Ops, SparseCore 0:
  11.7 27.9 all-gather.4
  41.9 55.8 all-gather.6
  100.0 59.9 all-gather.10
  183.2 39.2 all-gather.8
